TPU v7x, 8 devices: a whole 2x2x1 slice. The times are simulated.
8 devices in a mesh: dp: 2 (over z, y), tp: 4 (over x, core).
Axes of the slice: x: 2, y: 2, z: 1, core: 2. Of those that a mesh axis runs over, the one named last changes fastest.
Arguments:
- hidden_states: bfloat16 [1024, 4096], P(('dp', 'tp')), parts along dimension 0
- end_pos: int32 [512], P('dp'), parts along dimension 0
- is_final: int32 [512], P('dp'), parts along dimension 0
- norm_gain: float32 [4096], replicated
- w_head: bfloat16 [4096, 32000], P(None, 'tp')
Outputs:
- output 1: float32 [512, 32000], P('dp', 'tp'), parts along dimension 0
- output 2: float32 [512], P('dp'), parts along dimension 0
There are 2 independent parts. A program takes and returns all parts, laid end to end along the dimension named above; an argument that names none is the same for every part.
All inputs are finite; a program needn't handle non-finite values.
Results may differ from a plain program's by a relative error of at most 0.001.
Values are sent between devices in bfloat16 or wider.
A program may use at most 1 GiB of HBM per device.

v0:
```python
import jax
import jax.numpy as jnp
from jax import lax
from jax.sharding import PartitionSpec as P

NORM_EPS = 1e-5


def head_block(sel_rows, is_final, norm_gain, w_block):
    rows_f32 = sel_rows.astype(jnp.float32)
    inv_rms = lax.rsqrt(jnp.mean(rows_f32 * rows_f32, axis=1, keepdims=True) + NORM_EPS)
    normed = (rows_f32 * inv_rms * norm_gain[None, :]).astype(jnp.bfloat16)
    logits = jnp.dot(normed, w_block, preferred_element_type=jnp.float32)
    local_max = jnp.max(logits, axis=1)
    local_sum = jnp.sum(jnp.exp(logits - local_max[:, None]), axis=1)
    group_stats = lax.all_gather(jnp.stack([local_max, local_sum]), "tp")
    group_max = jnp.max(group_stats[:, 0], axis=0)
    total_sum = jnp.sum(group_stats[:, 1] * jnp.exp(group_stats[:, 0] - group_max[None, :]), axis=0)
    log_norm = group_max + jnp.log(total_sum)
    log_probs = jnp.where(is_final[:, None] == 1, logits - log_norm[:, None], 0.0)
    return log_probs, log_norm


def solution(mesh):
    def body(hidden_blk, end_pos, is_final, norm_gain, w_block):
        full_hidden = lax.all_gather(hidden_blk, "tp", axis=0, tiled=True)
        sel_rows = jnp.take(full_hidden, end_pos, axis=0)
        return head_block(sel_rows, is_final, norm_gain, w_block)

    return jax.shard_map(
        body,
        mesh=mesh,
        in_specs=(P(("dp", "tp"), None), P("dp"), P("dp"), P(None), P(None, "tp")),
        out_specs=(P("dp", "tp"), P("dp")),
        check_vma=False,
    )
```

profile of v0, /device:TPU:0, one launch (start us, length us, event | category | flops | bytes accessed | tf_op | source)
XLA Modules:
  0.0 96.2 jit_solution(6714334652417188248)
XLA Ops:
  7.2 0.0 all-gather.4.cloned.1.call-start
  7.2 0.7 all-gather.4.cloned.1.call-update
  7.9 0.7 compare_select_fusion
  8.6 0.7 compare_and_fusion
  9.3 0.7 broadcast_compare_fusion
  10.0 0.0 copy-start.1
  10.0 33.9 %all-gather.4.cloned.1.call-done = bf16[512,4096]{1,0:T(8,128)(2,1)} async-done(((bf16[128,4096]{1,0:T(8,128)(2,1)}), bf16[512,4096]{1,0:T(8,128)(2,1)}) %all-gather.4.cloned.1.call-update) | async-done | bytes 4194320 | tf_op jit(solution)/shard_map/all_gather | solution.py:26
  43.9 6.6 %gather_fusion = bf16[256,4096]{1,0:T(8,128)(2,1)S(1)} fusion(bf16[512,4096]{1,0:T(8,128)(2,1)} %all-gather.4.cloned.1.call-done, s32[1024]{0:T(1024)S(1)} %pad_clamp_fusion), kind=kCustom, calls=%fused_computation | custom fusion | bytes 4195328 | tf_op jit(solution)/shard_map/jit(_take)/gather | solution.py:27
  50.5 0.7 fusion
  51.2 0.0 copy-done.1
  51.2 26.2 %fusion.12 = (f32[256]{0:T(256)S(1)}, f32[256,8000]{0,1:T(8,128)S(1)}) fusion(bf16[4096,8000]{0,1:T(8,128)(2,1)} %param.9, f32[4096]{0:T(1024)S(1)} %copy-done.1, f32[256]{0:T(256)S(1)} %add_rsqrt_fusion, bf16[256,4096]{1,0:T(8,128)(2,1)S(1)} %gather_fusion, pred[256]{0:T(512)(128)(4,1)S(1)} %compare_and_fusion), kind=kOutput, calls=%fused_computation.27 | convolution fusion | flops 16784506880 | bytes 75843840 | tf_op jit(solution)/shard_map/dot_general | solution.py:13
  77.4 1.1 %exponential_reduce_fusion = f32[256]{0:T(256)S(1)} fusion(f32[256,8000]{0,1:T(8,128)S(1)} %get-tuple-element.6, f32[256]{0:T(256)S(1)} %get-tuple-element.5), kind=kLoop, calls=%fused_computation.2 | loop fusion | flops 4095744 | bytes 8194048 | tf_op jit(solution)/shard_map/reduce_sum | solution.py:15
  78.5 6.8 %all-gather.1 = f32[4,2,256]{2,1,0:T(2,128)S(1)} all-gather(f32[1,2,256]{2,1,0:T(2,128)S(1)} %maximum_bitcast_fusion), channel_id=2, replica_groups=mesh['dp'=2,'tp'=4] {'tp'}, dimensions={0}, use_global_device_ids=true | all-gather | bytes 10240 | tf_op jit(solution)/shard_map/all_gather | solution.py:16
  85.4 0.0 copy-start
  85.4 3.9 %subtract_select_fusion = f32[256,8000]{0,1:T(8,128)} fusion(f32[256,8000]{0,1:T(8,128)S(1)} %get-tuple-element.6, f32[256]{0:T(256)S(1)} %log_add_fusion, pred[256]{0:T(512)(128)(4,1)S(1)} %broadcast_compare_fusion), kind=kLoop, calls=%fused_computation.1 | loop fusion | flops 4096000 | bytes 16385280 | tf_op jit(solution)/shard_map/jit(_where)/select_n | solution.py:20
  89.3 0.0 copy-done
  (6 shorter events, 0.1 us)
Async XLA Ops:
  7.2 36.7 %all-gather.4.cloned.1.call-start = ((), (), s32[]{:S(2)}) async-start(), calls=%async_computation | async-start | bytes 5242880 | tf_op jit(solution)/shard_map/all_gather | solution.py:26
  10.0 41.2 %copy-start.1 = (f32[4096]{0:T(1024)S(1)}, f32[4096]{0:T(1024)}, u32[]{:S(2)}) copy-start(f32[4096]{0:T(1024)} %param.8) | copy-start | bytes 49156
  85.4 3.9 %copy-start = (f32[256]{0:T(256)}, f32[256]{0:T(256)S(1)}, u32[]{:S(2)}) copy-start(f32[256]{0:T(256)S(1)} %log_add_fusion) | copy-start | bytes 3076
Sparse Core Ops, SparseCore 0:
  9.5 34.3 all-gather.3
where the time goes:
time: 96.5 us; the launch traced here: 96.2 us
  waiting for transfers between devices  34.6 us (36%)
  matrix products  26.2 us (27%)
  between operations  14.1 us (15%)
  other arithmetic  7.86 us (8%)
  blocking collectives  6.82 us (7%)
  local copies, waits for them, and re-layouts  6.62 us (7%)
    all_gather x1, waiting for transfers between devices, body(): full_hidden = lax.all_gather(hidden_blk, 'tp', axis=0, tiled=True)  33.9 us
    dot_general x1, matrix products, head_block(): logits = jnp.dot(normed, w_block, preferred_element_type=jnp.float32)  26.2 us
    all_gather x1, blocking collectives, head_block(): group_stats = lax.all_gather(jnp.stack([local_max, local_sum]), 'tp')  6.82 us
    gather x1, local copies, waits for them, and re-layouts, body(): sel_rows = jnp.take(full_hidden, end_pos, axis=0)  6.61 us
    select_n x1, other arithmetic, head_block(): jnp.where(is_final[:, None] == 1, logits - log_norm[:, None], 0.0)  3.88 us
  transfers between devices with their start and end apart: 1, of which 1 were waited for; matrix products, arithmetic and copies ran while one was open for 2% of the time, Pallas kernels for 0%

commit v1 on v0

v1 whole, which is shorter than its diff:
```python
import functools

import jax
import jax.numpy as jnp
from jax import lax
from jax.experimental import pallas as pl
from jax.experimental.pallas import tpu as pltpu
from jax.sharding import PartitionSpec as P

NORM_EPS = 1e-5
MESH = pl.DeviceIdType.MESH
CW = 256
WK = 512
W_SLOTS = 5
W_PIECES = 4
ROWS_OUT = 1000


def gather_head_kernel(
    hidden_ref, pos_ref, gain_ref, w_ref, logits_ref, norm_ref,
    rows, w_ring, onehot, x_buf, inv_buf, stat_buf,
    own_sem, w_sem, xs_sem, xr_sem, ps_sem, pr_sem, fs_sem, fr_sem, is_sem, ir_sem, ss_sem, sr_sem,
):
    n_tok, hidden = hidden_ref.shape
    vocab = w_ref.shape[0]
    n_req = pos_ref.shape[1]
    n_slices = hidden // CW
    n_w = hidden // WK
    per_w = WK // CW
    dp, me = lax.axis_index("dp"), lax.axis_index("tp")
    across = lax.rem(me + 2, 4)
    partner = me + 1 - 2 * lax.rem(me, 2)
    corner = lax.rem(partner + 2, 4)
    peers = (across, partner, corner)

    def block(owner):
        return pl.ds(pl.multiple_of(owner * n_tok, n_tok), n_tok)

    def own_copy(j):
        return pltpu.make_async_copy(
            hidden_ref.at[:, pl.ds(j * CW, CW)], rows.at[j, block(me)], own_sem.at[j]
        )

    def w_copy(s, p):
        m = vocab // W_PIECES
        return pltpu.make_async_copy(
            w_ref.at[pl.ds(p * m, m), pl.ds(s * WK, WK)],
            w_ring.at[s % W_SLOTS, pl.ds(p * m, m)],
            w_sem.at[s % W_SLOTS, p],
        )

    def send_rows(j, owner, send, recv, target):
        return pltpu.make_async_remote_copy(
            src_ref=rows.at[j, block(owner)], dst_ref=rows.at[j, block(owner)],
            send_sem=send.at[j], recv_sem=recv.at[j],
            device_id=(dp, target), device_id_type=MESH,
        )

    def to_across(j):
        return send_rows(j, me, xs_sem, xr_sem, across)

    def to_partner(j):
        return send_rows(j, me, ps_sem, pr_sem, partner)

    def forward(j):
        return send_rows(j, across, fs_sem, fr_sem, partner)

    def send_small(buf, i, send, recv):
        return pltpu.make_async_remote_copy(
            src_ref=buf.at[me], dst_ref=buf.at[me], send_sem=send.at[i], recv_sem=recv.at[i],
            device_id=(dp, peers[i]), device_id_type=MESH,
        )

    for j in range(n_slices):
        own_copy(j).start()
    for s in range(min(W_SLOTS, n_w)):
        for p in range(W_PIECES):
            w_copy(s, p).start()

    barrier = pltpu.get_barrier_semaphore()
    for peer in peers:
        pl.semaphore_signal(barrier, inc=1, device_id=(dp, peer), device_id_type=MESH)
    pl.semaphore_wait(barrier, 3)

    early = 3
    for j in range(early):
        own_copy(j).wait()
        to_across(j).start()
        to_partner(j).start()
    for j in range(early, n_slices):
        own_copy(j).wait()
        to_partner(j).start()
    total = jnp.zeros((n_tok, CW), jnp.float32)
    for j in range(n_slices):
        r = rows[j, block(me)].astype(jnp.float32)
        total += r * r
    inv = lax.rsqrt(jnp.sum(total, axis=1, keepdims=True) * (1.0 / hidden) + NORM_EPS)
    eye = lax.broadcasted_iota(jnp.int32, (n_tok, n_tok), 0) == lax.broadcasted_iota(jnp.int32, (n_tok, n_tok), 1)
    inv_row = jnp.sum(jnp.where(eye, inv, 0.0), axis=0, keepdims=True)
    inv_buf[me] = jnp.broadcast_to(inv_row, inv_buf.shape[1:])
    picks = lax.broadcasted_iota(jnp.int32, (4 * n_tok, n_req), 0) == pos_ref[...]
    onehot[...] = jnp.where(picks, 1.0, 0.0).T.astype(jnp.bfloat16)
    for i in range(3):
        send_small(inv_buf, i, is_sem, ir_sem).start()
    for j in range(early, n_slices):
        to_across(j).start()

    for i in range(3):
        send_small(inv_buf, i, is_sem, ir_sem).wait_recv()
    inv_sel = jnp.zeros((n_req, 1), jnp.float32)
    for o in range(4):
        hit = onehot[:, o * n_tok:(o + 1) * n_tok].astype(jnp.float32)
        inv_sel += jnp.sum(hit * inv_buf[o, 0:1, :], axis=1, keepdims=True)

    def prepare(j, k):
        to_partner(j).wait_recv()
        forward(j).wait_recv()
        r = jnp.dot(onehot[...], rows[j], preferred_element_type=jnp.float32)
        x_buf[:, k * CW:(k + 1) * CW] = (r * inv_sel * gain_ref[:, j * CW:(j + 1) * CW]).astype(jnp.bfloat16)

    def relay(j):
        to_across(j).wait_recv()
        forward(j).start()

    steps = [tuple(range(s * per_w, (s + 1) * per_w)) for s in range(n_w - 1)]
    steps += [(j,) for j in range((n_w - 1) * per_w, n_w * per_w)]
    mb = vocab // 2
    for j in steps[0]:
        relay(j)
    run_max = jnp.full((1, n_req), -jnp.inf, jnp.float32)
    run_sum = jnp.zeros((1, n_req), jnp.float32)
    for i, cols in enumerate(steps):
        if i + 1 < len(steps):
            for j in steps[i + 1]:
                relay(j)
        for k, j in enumerate(cols):
            prepare(j, k)
        s, width = cols[0] // per_w, len(cols) * CW
        off = (cols[0] % per_w) * CW
        if off == 0:
            for p in range(W_PIECES):
                w_copy(s, p).wait()
        first, last = i == 0, i + 1 == len(steps)

        def body(m, carry):
            at = pl.ds(pl.multiple_of(m * mb, 8), mb)
            z = lax.dot_general(
                w_ring[s % W_SLOTS, at, off:off + width], x_buf[:, :width],
                (((1,), (1,)), ((), ())), preferred_element_type=jnp.float32,
            )
            if not first:
                z += logits_ref[at, :]
            logits_ref[at, :] = z
            return carry

        lax.fori_loop(0, vocab // mb, body, 0)
        if off + width == WK and s + W_SLOTS < n_w:
            for p in range(W_PIECES):
                w_copy(s + W_SLOTS, p).start()

    sb = ROWS_OUT

    def stat_body(m, carry):
        run_max, run_sum = carry
        z = logits_ref[pl.ds(pl.multiple_of(m * sb, 8), sb), :]
        new_max = jnp.maximum(run_max, jnp.max(z, axis=0, keepdims=True))
        run_sum = run_sum * jnp.exp(run_max - new_max) + jnp.sum(jnp.exp(z - new_max), axis=0, keepdims=True)
        return new_max, run_sum

    run_max, run_sum = lax.fori_loop(0, vocab // sb, stat_body, (run_max, run_sum))
    stat_buf[me, 0:1, :] = run_max
    stat_buf[me, 1:2, :] = run_sum
    for i in range(3):
        send_small(stat_buf, i, ss_sem, sr_sem).start()
    for j in range(n_slices):
        to_across(j).wait_send()
        to_partner(j).wait_send()
        forward(j).wait_send()
    for i in range(3):
        send_small(inv_buf, i, is_sem, ir_sem).wait_send()
    for i in range(3):
        send_small(stat_buf, i, ss_sem, sr_sem).wait()
    group_max = jnp.max(stat_buf[:, 0, :], axis=0, keepdims=True)
    group_sum = jnp.sum(stat_buf[:, 1, :] * jnp.exp(stat_buf[:, 0, :] - group_max), axis=0, keepdims=True)
    norm_ref[...] = group_max + jnp.log(group_sum)


def finish_kernel(logits_ref, norm_ref, flag_ref, out_ref, norm_out_ref, stage, sem):
    vocab = logits_ref.shape[0]
    n = vocab // ROWS_OUT
    keep = flag_ref[...] == 1
    norm = norm_ref[...]
    norm_out_ref[...] = norm

    def out_copy(m):
        at = pl.ds(m * ROWS_OUT, ROWS_OUT)
        return pltpu.make_async_copy(stage.at[at], out_ref.at[at], sem.at[m])

    for m in range(n):
        at = pl.ds(m * ROWS_OUT, ROWS_OUT)
        stage[at, :] = jnp.where(keep, logits_ref[at, :] - norm, 0.0)
        out_copy(m).start()
    for m in range(n):
        out_copy(m).wait()


def solution(mesh):
    def body(hidden_blk, end_pos, is_final, norm_gain, w_block):
        n_tok, hidden = hidden_blk.shape
        vocab = w_block.shape[1]
        n_req = end_pos.shape[0]
        n_slices = hidden // CW
        f32 = jnp.float32
        vmem = pl.BlockSpec(memory_space=pltpu.VMEM)
        hbm = pl.BlockSpec(memory_space=pl.ANY)
        dma = pltpu.SemaphoreType.DMA
        logits, norm = pl.pallas_call(
            gather_head_kernel,
            out_shape=(pltpu.VMEM((vocab, n_req), f32), pltpu.VMEM((1, n_req), f32)),
            in_specs=[hbm, vmem, vmem, hbm],
            out_specs=(vmem, vmem),
            scratch_shapes=[
                pltpu.VMEM((n_slices, 4 * n_tok, CW), jnp.bfloat16),
                pltpu.VMEM((W_SLOTS, vocab, WK), jnp.bfloat16),
                pltpu.VMEM((n_req, 4 * n_tok), jnp.bfloat16),
                pltpu.VMEM((n_req, WK), jnp.bfloat16),
                pltpu.VMEM((4, 8, n_tok), f32),
                pltpu.VMEM((4, 8, n_req), f32),
                dma((n_slices,)), dma((W_SLOTS, W_PIECES)),
                dma((n_slices,)), dma((n_slices,)), dma((n_slices,)), dma((n_slices,)),
                dma((n_slices,)), dma((n_slices,)), dma((3,)), dma((3,)), dma((3,)), dma((3,)),
            ],
            compiler_params=pltpu.CompilerParams(
                collective_id=0, has_side_effects=True, vmem_limit_bytes=54 * 1024 * 1024
            ),
            name="gather_head",
        )(hidden_blk, end_pos.reshape(1, n_req), norm_gain.reshape(1, hidden), w_block.T)
        out, log_norm = pl.pallas_call(
            finish_kernel,
            out_shape=(jax.ShapeDtypeStruct((vocab, n_req), f32), jax.ShapeDtypeStruct((1, n_req), f32)),
            in_specs=[vmem, vmem, vmem],
            out_specs=(hbm, vmem),
            scratch_shapes=[pltpu.VMEM((vocab, n_req), f32), dma((vocab // ROWS_OUT,))],
            compiler_params=pltpu.CompilerParams(vmem_limit_bytes=20 * 1024 * 1024),
            name="finish",
        )(logits, norm, is_final.reshape(1, n_req))
        return out.T, log_norm.reshape(n_req)

    return jax.shard_map(
        body,
        mesh=mesh,
        in_specs=(P(("dp", "tp"), None), P("dp"), P("dp"), P(None), P(None, "tp")),
        out_specs=(P("dp", "tp"), P("dp")),
        check_vma=False,
    )
```

time: 96.5 us -> 55.1 us (0.57)
  Pallas kernels: 0 us -> 54.3 us
  waiting for transfers between devices: 34.6 us -> 0 us
  matrix products: 26.2 us -> 0 us
  between operations: 14.1 us -> 0.65 us
  other arithmetic: 7.86 us -> 0 us
  blocking collectives: 6.82 us -> 0 us
  local copies, waits for them, and re-layouts: 6.62 us -> 0.01 us
    pallas_call x0 -> x2, Pallas kernels: none -> 54.3 us  [the longest x1 50.3 us: body(): pl.pallas_call(gather_head_kernel, out_shape=(pltpu.VMEM((vocab, n_req),...]
    all_gather x1 -> x0, waiting for transfers between devices: 33.9 us -> none  [body(): full_hidden = lax.all_gather(hidden_blk, 'tp', axis=0, tiled=True)]
    dot_general x1 -> x0, matrix products: 26.2 us -> none  [head_block(): logits = jnp.dot(normed, w_block, preferred_element_type=jnp.float32)]
    all_gather x1 -> x0, blocking collectives: 6.82 us -> none  [head_block(): group_stats = lax.all_gather(jnp.stack([local_max, local_sum]), 'tp')]
    gather x1 -> x0, local copies, waits for them, and re-layouts: 6.61 us -> none  [body(): sel_rows = jnp.take(full_hidden, end_pos, axis=0)]
    select_n x2 -> x0, other arithmetic: 4.57 us -> none  [the longest x1 3.88 us: head_block(): jnp.where(is_final[:, None] == 1, logits - log_norm[:, None], 0.0)]
    reduce_sum x3 -> x0, other arithmetic: 1.87 us -> none  [the longest x1 1.14 us: head_block(): local_sum = jnp.sum(jnp.exp(logits - local_max[:, None]), axis=1)]
  transfers between devices with their start and end apart: 1 -> 0, of which waited for: 1 -> 0; matrix products, arithmetic and copies ran while one was open for 2% -> 0% of each run, Pallas kernels for 0% -> 0%
where the time goes in v1:
time: 55.1 us; the launch traced here: 54.9 us
  Pallas kernels  54.3 us (99%)
  between operations  0.65 us (1%)
    pallas_call x1, Pallas kernels, body(): pl.pallas_call(gather_head_kernel, out_shape=(pltpu.VMEM((vocab, n_req),...  50.3 us
    pallas_call x1, Pallas kernels, body(): pl.pallas_call(finish_kernel, out_shape=(jax.ShapeDtypeStruct((vocab, n_r...  3.96 us

profile of v1, /device:TPU:0, one launch (start us, length us, event | category | flops | bytes accessed | tf_op | source)
XLA Modules:
  0.0 54.9 jit_solution(1685948077298185734)
XLA Ops:
  0.6 0.0 copy-start
  0.6 50.3 %gather_head.1 = (f32[8000,256]{1,0:T(8,128)S(1)}, f32[1,256]{1,0:T(1,128)S(1)}) custom-call(bf16[128,4096]{1,0:T(8,128)(2,1)} %hidden_ref.1, s32[1,256]{1,0:T(1,128)} %bitcast.9, f32[1,4096]{1,0:T(1,128)} %bitcast.8, bf16[8000,4096]{1,0:T(8,128)(2,1)} %bitcast.7), custom_call_target="tpu_custom_call" | custom-call | tf_op jit(solution)/shard_map/gather_head/pallas_call | solution.py:217
  51.0 0.0 copy-done
  51.0 4.0 %finish.1 = (f32[8000,256]{1,0:T(8,128)}, f32[1,256]{1,0:T(1,128)}) custom-call(f32[8000,256]{1,0:T(8,128)S(1)} %get-tuple-element.6.logits_ref, f32[1,256]{1,0:T(1,128)S(1)} %get-tuple-element.7.norm_ref, s32[1,256]{1,0:T(1,128)S(1)} %bitcast.6), custom_call_target="tpu_custom_call" | custom-call | tf_op jit(solution)/shard_map/finish/pallas_call | solution.py:238
Async XLA Ops:
  0.6 50.3 %copy-start = (s32[256]{0:T(256)S(1)}, s32[256]{0:T(256)}, u32[]{:S(2)}) copy-start(s32[256]{0:T(256)} %param.7) | copy-start | bytes 3076

commit v2 on v1

--- a/solution.py
+++ b/solution.py
@@ -75,7 +75,7 @@
         own_copy(j).start()
     for s in range(min(W_SLOTS, n_w)):
         for p in range(W_PIECES):
-            w_copy(s, p).start()
+            w_copy(s, p).start(priority=1)
 
     barrier = pltpu.get_barrier_semaphore()
     for peer in peers:
@@ -156,7 +156,7 @@
         lax.fori_loop(0, vocab // mb, body, 0)
         if off + width == WK and s + W_SLOTS < n_w:
             for p in range(W_PIECES):
-                w_copy(s + W_SLOTS, p).start()
+                w_copy(s + W_SLOTS, p).start(priority=1)
 
     sb = ROWS_OUT
 

time: 55.1 us -> 48.7 us (0.88)
  Pallas kernels: 54.3 us -> 47.8 us
    pallas_call x1, Pallas kernels: 50.3 us -> 43.8 us  [body(): pl.pallas_call(gather_head_kernel, out_shape=(pltpu.VMEM((vocab, n_req),...]
where the time goes in v2:
time: 48.7 us; the launch traced here: 48.5 us
  Pallas kernels  47.8 us (98%)
  between operations  0.65 us (1%)
    pallas_call x1, Pallas kernels, body(): pl.pallas_call(gather_head_kernel, out_shape=(pltpu.VMEM((vocab, n_req),...  43.8 us
    pallas_call x1, Pallas kernels, body(): pl.pallas_call(finish_kernel, out_shape=(jax.ShapeDtypeStruct((vocab, n_r...  3.96 us

profile of v2, /device:TPU:0, one launch (start us, length us, event | category | flops | bytes accessed | tf_op | source)
XLA Modules:
  0.0 48.5 jit_solution(12362536021525605859)
XLA Ops:
  0.6 0.0 copy-start
  0.6 43.8 %gather_head.1 = (f32[8000,256]{1,0:T(8,128)S(1)}, f32[1,256]{1,0:T(1,128)S(1)}) custom-call(bf16[128,4096]{1,0:T(8,128)(2,1)} %hidden_ref.1, s32[1,256]{1,0:T(1,128)} %bitcast.9, f32[1,4096]{1,0:T(1,128)} %bitcast.8, bf16[8000,4096]{1,0:T(8,128)(2,1)} %bitcast.7), custom_call_target="tpu_custom_call" | custom-call | tf_op jit(solution)/shard_map/gather_head/pallas_call | solution.py:217
  44.5 0.0 copy-done
  44.5 4.0 %finish.1 = (f32[8000,256]{1,0:T(8,128)}, f32[1,256]{1,0:T(1,128)}) custom-call(f32[8000,256]{1,0:T(8,128)S(1)} %get-tuple-element.6.logits_ref, f32[1,256]{1,0:T(1,128)S(1)} %get-tuple-element.7.norm_ref, s32[1,256]{1,0:T(1,128)S(1)} %bitcast.6), custom_call_target="tpu_custom_call" | custom-call | tf_op jit(solution)/shard_map/finish/pallas_call | solution.py:238
Async XLA Ops:
  0.6 43.9 %copy-start = (s32[256]{0:T(256)S(1)}, s32[256]{0:T(256)}, u32[]{:S(2)}) copy-start(s32[256]{0:T(256)} %param.7) | copy-start | bytes 3076

commit v3 on v2

--- a/solution.py
+++ b/solution.py
@@ -14,12 +14,15 @@
 W_SLOTS = 5
 W_PIECES = 4
 ROWS_OUT = 1000
+CUTS = {2: (3200, 6400), 1: (3200, 4800)}
+EDGES = (0, 2400, 4800, 6400, 7360, 8000)
+SPLITS = {-1: (1, 1)}
 
 
 def gather_head_kernel(
-    hidden_ref, pos_ref, gain_ref, w_ref, logits_ref, norm_ref,
-    rows, w_ring, onehot, x_buf, inv_buf, stat_buf,
-    own_sem, w_sem, xs_sem, xr_sem, ps_sem, pr_sem, fs_sem, fr_sem, is_sem, ir_sem, ss_sem, sr_sem,
+    hidden_ref, pos_hbm, gain_hbm, w_ref, logits_ref, norm_ref,
+    rows, w_ring, onehot, x_buf, inv_buf, stat_buf, pos_ref, gain_ref,
+    own_sem, w_sem, in_sem, xs_sem, xr_sem, ps_sem, pr_sem, fs_sem, fr_sem, is_sem, ir_sem, ss_sem, sr_sem,
 ):
     n_tok, hidden = hidden_ref.shape
     vocab = w_ref.shape[0]
@@ -33,6 +36,10 @@
     corner = lax.rem(partner + 2, 4)
     peers = (across, partner, corner)
 
+    barrier = pltpu.get_barrier_semaphore()
+    for peer in peers:
+        pl.semaphore_signal(barrier, inc=1, device_id=(dp, peer), device_id_type=MESH)
+
     def block(owner):
         return pl.ds(pl.multiple_of(owner * n_tok, n_tok), n_tok)
 
@@ -71,18 +78,20 @@
             device_id=(dp, peers[i]), device_id_type=MESH,
         )
 
+    small = (
+        pltpu.make_async_copy(pos_hbm, pos_ref, in_sem.at[0]),
+        pltpu.make_async_copy(gain_hbm, gain_ref, in_sem.at[1]),
+    )
     for j in range(n_slices):
         own_copy(j).start()
+    for copy in small:
+        copy.start()
     for s in range(min(W_SLOTS, n_w)):
         for p in range(W_PIECES):
             w_copy(s, p).start(priority=1)
-
-    barrier = pltpu.get_barrier_semaphore()
-    for peer in peers:
-        pl.semaphore_signal(barrier, inc=1, device_id=(dp, peer), device_id_type=MESH)
     pl.semaphore_wait(barrier, 3)
 
-    early = 3
+    early = 2
     for j in range(early):
         own_copy(j).wait()
         to_across(j).start()
@@ -98,6 +107,8 @@
     eye = lax.broadcasted_iota(jnp.int32, (n_tok, n_tok), 0) == lax.broadcasted_iota(jnp.int32, (n_tok, n_tok), 1)
     inv_row = jnp.sum(jnp.where(eye, inv, 0.0), axis=0, keepdims=True)
     inv_buf[me] = jnp.broadcast_to(inv_row, inv_buf.shape[1:])
+    for copy in small:
+        copy.wait()
     picks = lax.broadcasted_iota(jnp.int32, (4 * n_tok, n_req), 0) == pos_ref[...]
     onehot[...] = jnp.where(picks, 1.0, 0.0).T.astype(jnp.bfloat16)
     for i in range(3):
@@ -112,64 +123,116 @@
         hit = onehot[:, o * n_tok:(o + 1) * n_tok].astype(jnp.float32)
         inv_sel += jnp.sum(hit * inv_buf[o, 0:1, :], axis=1, keepdims=True)
 
-    def prepare(j, k):
-        to_partner(j).wait_recv()
-        forward(j).wait_recv()
-        r = jnp.dot(onehot[...], rows[j], preferred_element_type=jnp.float32)
-        x_buf[:, k * CW:(k + 1) * CW] = (r * inv_sel * gain_ref[:, j * CW:(j + 1) * CW]).astype(jnp.bfloat16)
-
     def relay(j):
         to_across(j).wait_recv()
         forward(j).start()
 
-    steps = [tuple(range(s * per_w, (s + 1) * per_w)) for s in range(n_w - 1)]
-    steps += [(j,) for j in range((n_w - 1) * per_w, n_w * per_w)]
-    mb = vocab // 2
+    def arrived(j):
+        to_partner(j).wait_recv()
+        forward(j).wait_recv()
+
+    def prepare(j, k, slot):
+        r = jnp.dot(onehot[...], rows[j], preferred_element_type=jnp.float32)
+        x = r * inv_sel * gain_ref[:, j * CW:(j + 1) * CW]
+        x_buf[slot, :, k * CW:(k + 1) * CW] = x.astype(jnp.bfloat16)
+
+    steps = []
+    for s in range(n_w):
+        for width in SPLITS.get(s - n_w, SPLITS.get(s, (per_w,))):
+            first = steps[-1][-1] + 1 if steps else 0
+            steps.append(tuple(range(first, first + width)))
+
+    once = 1 + me // 4
+
+    def alone(work, *carry):
+        return lax.fori_loop(0, once, lambda k, c: work(*c), carry)
+
+    def multiply(i, start, size):
+        cols = steps[i]
+        off, width = cols[0] % per_w * CW, len(cols) * CW
+        z = lax.dot_general(
+            w_ring[cols[0] // per_w % W_SLOTS, start:start + size, off:off + width], x_buf[i % 2, :, :width],
+            (((1,), (1,)), ((), ())), preferred_element_type=jnp.float32,
+        )
+        if i > 0:
+            z += logits_ref[start:start + size, :]
+        logits_ref[start:start + size, :] = z
+        return z
+
+    def piece(i, start, stop, extra=None):
+        if start == stop:
+            return
+
+        def work():
+            if extra is not None:
+                extra()
+            multiply(i, start, stop - start)
+            return ()
+
+        alone(work)
+
+    lanes = 4 * 8
+
+    def highest(z, run_max):
+        return jnp.maximum(run_max, jnp.max(z.reshape(z.shape[0] // lanes, lanes, n_req), axis=0))
+
+    def add_up(start, stop, run_max, ref, run_sum):
+        z = logits_ref[start:stop, :].reshape((stop - start) // lanes, lanes, n_req)
+        return run_sum * jnp.exp(ref - run_max) + jnp.sum(jnp.exp(z - run_max), axis=0)
+
+    def w_wait(s):
+        for p in range(W_PIECES):
+            w_copy(s, p).wait()
+
+    last = len(steps) - 1
     for j in steps[0]:
         relay(j)
-    run_max = jnp.full((1, n_req), -jnp.inf, jnp.float32)
-    run_sum = jnp.zeros((1, n_req), jnp.float32)
-    for i, cols in enumerate(steps):
-        if i + 1 < len(steps):
-            for j in steps[i + 1]:
+    for k, j in enumerate(steps[0]):
+        arrived(j)
+        prepare(j, k, 0)
+    w_wait(0)
+    pending = [j for cols in steps[1:] for j in cols]
+    for i in range(last):
+        cols, nxt = steps[i], steps[i + 1]
+        cut_1, cut_2 = CUTS[len(cols)]
+        piece(i, 0, cut_1)
+        for j in nxt:
+            if j in pending:
                 relay(j)
-        for k, j in enumerate(cols):
-            prepare(j, k)
-        s, width = cols[0] // per_w, len(cols) * CW
-        off = (cols[0] % per_w) * CW
-        if off == 0:
-            for p in range(W_PIECES):
-                w_copy(s, p).wait()
-        first, last = i == 0, i + 1 == len(steps)
-
-        def body(m, carry):
-            at = pl.ds(pl.multiple_of(m * mb, 8), mb)
-            z = lax.dot_general(
-                w_ring[s % W_SLOTS, at, off:off + width], x_buf[:, :width],
-                (((1,), (1,)), ((), ())), preferred_element_type=jnp.float32,
-            )
-            if not first:
-                z += logits_ref[at, :]
-            logits_ref[at, :] = z
-            return carry
-
-        lax.fori_loop(0, vocab // mb, body, 0)
-        if off + width == WK and s + W_SLOTS < n_w:
-            for p in range(W_PIECES):
-                w_copy(s + W_SLOTS, p).start(priority=1)
-
-    sb = ROWS_OUT
-
-    def stat_body(m, carry):
-        run_max, run_sum = carry
-        z = logits_ref[pl.ds(pl.multiple_of(m * sb, 8), sb), :]
-        new_max = jnp.maximum(run_max, jnp.max(z, axis=0, keepdims=True))
-        run_sum = run_sum * jnp.exp(run_max - new_max) + jnp.sum(jnp.exp(z - new_max), axis=0, keepdims=True)
-        return new_max, run_sum
-
-    run_max, run_sum = lax.fori_loop(0, vocab // sb, stat_body, (run_max, run_sum))
-    stat_buf[me, 0:1, :] = run_max
-    stat_buf[me, 1:2, :] = run_sum
+                pending.remove(j)
+        piece(i, cut_1, cut_2)
+        if len(nxt) == 1 and i + 2 <= last:
+            for j in steps[i + 2]:
+                relay(j)
+                pending.remove(j)
+        for j in nxt:
+            arrived(j)
+
+        def prepare_next():
+            for k, j in enumerate(nxt):
+                prepare(j, k, (i + 1) % 2)
+
+        piece(i, cut_2, vocab, prepare_next)
+        s = cols[0] // per_w
+        if nxt[0] // per_w != s:
+            if s + W_SLOTS < n_w:
+                for p in range(W_PIECES):
+                    w_copy(s + W_SLOTS, p).start(priority=1)
+            w_wait(s + 1)
+    low = jnp.full((lanes, n_req), -jnp.inf, jnp.float32)
+    run_max, = alone(lambda m: (highest(multiply(last, EDGES[0], EDGES[1]), m),), low)
+    ref, run_sum = run_max, jnp.zeros((lanes, n_req), jnp.float32)
+    for k in range(1, len(EDGES) - 1):
+        def final(run_max, ref, run_sum):
+            z = multiply(last, EDGES[k], EDGES[k + 1] - EDGES[k])
+            run_sum = add_up(EDGES[k - 1], EDGES[k], run_max, ref, run_sum)
+            return highest(z, run_max), run_max, run_sum
+
+        run_max, ref, run_sum = alone(final, run_max, ref, run_sum)
+    run_sum = add_up(EDGES[-2], EDGES[-1], run_max, ref, run_sum)
+    local_max = jnp.max(run_max, axis=0, keepdims=True)
+    stat_buf[me, 0:1, :] = local_max
+    stat_buf[me, 1:2, :] = jnp.sum(run_sum * jnp.exp(run_max - local_max), axis=0, keepdims=True)
     for i in range(3):
         send_small(stat_buf, i, ss_sem, sr_sem).start()
     for j in range(n_slices):
@@ -217,16 +280,18 @@
         logits, norm = pl.pallas_call(
             gather_head_kernel,
             out_shape=(pltpu.VMEM((vocab, n_req), f32), pltpu.VMEM((1, n_req), f32)),
-            in_specs=[hbm, vmem, vmem, hbm],
+            in_specs=[hbm, hbm, hbm, hbm],
             out_specs=(vmem, vmem),
             scratch_shapes=[
                 pltpu.VMEM((n_slices, 4 * n_tok, CW), jnp.bfloat16),
                 pltpu.VMEM((W_SLOTS, vocab, WK), jnp.bfloat16),
                 pltpu.VMEM((n_req, 4 * n_tok), jnp.bfloat16),
-                pltpu.VMEM((n_req, WK), jnp.bfloat16),
+                pltpu.VMEM((2, n_req, WK), jnp.bfloat16),
                 pltpu.VMEM((4, 8, n_tok), f32),
                 pltpu.VMEM((4, 8, n_req), f32),
-                dma((n_slices,)), dma((W_SLOTS, W_PIECES)),
+                pltpu.VMEM((1, n_req), jnp.int32),
+                pltpu.VMEM((1, hidden), f32),
+                dma((n_slices,)), dma((W_SLOTS, W_PIECES)), dma((2,)),
                 dma((n_slices,)), dma((n_slices,)), dma((n_slices,)), dma((n_slices,)),
                 dma((n_slices,)), dma((n_slices,)), dma((3,)), dma((3,)), dma((3,)), dma((3,)),
             ],

time: 48.7 us -> 44.5 us (0.914)
  Pallas kernels: 47.8 us -> 43.6 us
    pallas_call x1, Pallas kernels: 43.8 us -> 39.6 us  [body(): pl.pallas_call(gather_head_kernel, out_shape=(pltpu.VMEM((vocab, n_req),...]
where the time goes in v3:
time: 44.5 us; the launch traced here: 44.4 us
  Pallas kernels  43.6 us (98%)
  between operations  0.82 us (2%)
    pallas_call x1, Pallas kernels, body(): pl.pallas_call(gather_head_kernel, out_shape=(pltpu.VMEM((vocab, n_req),...  39.6 us
    pallas_call x1, Pallas kernels, body(): pl.pallas_call(finish_kernel, out_shape=(jax.ShapeDtypeStruct((vocab, n_r...  3.96 us

profile of v3, /device:TPU:0, one launch (start us, length us, event | category | flops | bytes accessed | tf_op | source)
XLA Modules:
  0.0 44.4 jit_solution(7906731793803102567)
XLA Ops:
  0.6 0.0 copy-start
  0.6 39.6 %gather_head.1 = (f32[8000,256]{1,0:T(8,128)S(1)}, f32[1,256]{1,0:T(1,128)S(1)}) custom-call(bf16[128,4096]{1,0:T(8,128)(2,1)} %hidden_ref.1, s32[1,256]{1,0:T(1,128)} %bitcast.9, f32[1,4096]{1,0:T(1,128)} %bitcast.8, bf16[8000,4096]{1,0:T(8,128)(2,1)} %bitcast.7), custom_call_target="tpu_custom_call" | custom-call | tf_op jit(solution)/shard_map/gather_head/pallas_call | solution.py:280
  40.3 0.0 copy-done
  40.3 4.0 %finish.1 = (f32[8000,256]{1,0:T(8,128)}, f32[1,256]{1,0:T(1,128)}) custom-call(f32[8000,256]{1,0:T(8,128)S(1)} %get-tuple-element.6.logits_ref, f32[1,256]{1,0:T(1,128)S(1)} %get-tuple-element.7.norm_ref, s32[1,256]{1,0:T(1,128)S(1)} %bitcast.6), custom_call_target="tpu_custom_call" | custom-call | tf_op jit(solution)/shard_map/finish/pallas_call | solution.py:303
Async XLA Ops:
  0.6 39.6 %copy-start = (s32[256]{0:T(256)S(1)}, s32[256]{0:T(256)}, u32[]{:S(2)}) copy-start(s32[256]{0:T(256)} %param.7) | copy-start | bytes 3076

commit v4 on v3

--- a/solution.py
+++ b/solution.py
@@ -1,5 +1,3 @@
-import functools
-
 import jax
 import jax.numpy as jnp
 from jax import lax
@@ -14,9 +12,7 @@
 W_SLOTS = 5
 W_PIECES = 4
 ROWS_OUT = 1000
-CUTS = {2: (3200, 6400), 1: (3200, 4800)}
-EDGES = (0, 2400, 4800, 6400, 7360, 8000)
-SPLITS = {-1: (1, 1)}
+LAST = 800
 
 
 def gather_head_kernel(
@@ -91,14 +87,11 @@
             w_copy(s, p).start(priority=1)
     pl.semaphore_wait(barrier, 3)
 
-    early = 2
-    for j in range(early):
+    own_copy(0).wait()
+    to_across(0).start()
+    to_partner(0).start()
+    for j in range(1, n_slices):
         own_copy(j).wait()
-        to_across(j).start()
-        to_partner(j).start()
-    for j in range(early, n_slices):
-        own_copy(j).wait()
-        to_partner(j).start()
     total = jnp.zeros((n_tok, CW), jnp.float32)
     for j in range(n_slices):
         r = rows[j, block(me)].astype(jnp.float32)
@@ -107,15 +100,22 @@
     eye = lax.broadcasted_iota(jnp.int32, (n_tok, n_tok), 0) == lax.broadcasted_iota(jnp.int32, (n_tok, n_tok), 1)
     inv_row = jnp.sum(jnp.where(eye, inv, 0.0), axis=0, keepdims=True)
     inv_buf[me] = jnp.broadcast_to(inv_row, inv_buf.shape[1:])
+    for j in range(1, n_slices):
+        to_partner(j).start()
+    for i in range(3):
+        send_small(inv_buf, i, is_sem, ir_sem).start()
+    for j in range(1, n_slices):
+        to_across(j).start()
     for copy in small:
         copy.wait()
     picks = lax.broadcasted_iota(jnp.int32, (4 * n_tok, n_req), 0) == pos_ref[...]
     onehot[...] = jnp.where(picks, 1.0, 0.0).T.astype(jnp.bfloat16)
-    for i in range(3):
-        send_small(inv_buf, i, is_sem, ir_sem).start()
-    for j in range(early, n_slices):
-        to_across(j).start()
-
+
+    def relay(j):
+        to_across(j).wait_recv()
+        forward(j).start()
+
+    relay(0)
     for i in range(3):
         send_small(inv_buf, i, is_sem, ir_sem).wait_recv()
     inv_sel = jnp.zeros((n_req, 1), jnp.float32)
@@ -123,10 +123,6 @@
         hit = onehot[:, o * n_tok:(o + 1) * n_tok].astype(jnp.float32)
         inv_sel += jnp.sum(hit * inv_buf[o, 0:1, :], axis=1, keepdims=True)
 
-    def relay(j):
-        to_across(j).wait_recv()
-        forward(j).start()
-
     def arrived(j):
         to_partner(j).wait_recv()
         forward(j).wait_recv()
@@ -136,100 +132,76 @@
         x = r * inv_sel * gain_ref[:, j * CW:(j + 1) * CW]
         x_buf[slot, :, k * CW:(k + 1) * CW] = x.astype(jnp.bfloat16)
 
-    steps = []
-    for s in range(n_w):
-        for width in SPLITS.get(s - n_w, SPLITS.get(s, (per_w,))):
-            first = steps[-1][-1] + 1 if steps else 0
-            steps.append(tuple(range(first, first + width)))
-
+    steps = [tuple(range(s * per_w, (s + 1) * per_w)) for s in range(n_w)]
     once = 1 + me // 4
 
     def alone(work, *carry):
         return lax.fori_loop(0, once, lambda k, c: work(*c), carry)
 
-    def multiply(i, start, size):
-        cols = steps[i]
-        off, width = cols[0] % per_w * CW, len(cols) * CW
+    def multiply(i, start, size, lo=0, hi=WK):
+        at = pl.ds(start, size)
         z = lax.dot_general(
-            w_ring[cols[0] // per_w % W_SLOTS, start:start + size, off:off + width], x_buf[i % 2, :, :width],
+            w_ring[i % W_SLOTS, at, lo:hi], x_buf[i % 2, :, lo:hi],
             (((1,), (1,)), ((), ())), preferred_element_type=jnp.float32,
         )
-        if i > 0:
-            z += logits_ref[start:start + size, :]
-        logits_ref[start:start + size, :] = z
+        if i > 0 or lo > 0:
+            z += logits_ref[at, :]
+        logits_ref[at, :] = z
         return z
-
-    def piece(i, start, stop, extra=None):
-        if start == stop:
-            return
-
-        def work():
-            if extra is not None:
-                extra()
-            multiply(i, start, stop - start)
-            return ()
-
-        alone(work)
 
     lanes = 4 * 8
 
     def highest(z, run_max):
         return jnp.maximum(run_max, jnp.max(z.reshape(z.shape[0] // lanes, lanes, n_req), axis=0))
-
-    def add_up(start, stop, run_max, ref, run_sum):
-        z = logits_ref[start:stop, :].reshape((stop - start) // lanes, lanes, n_req)
-        return run_sum * jnp.exp(ref - run_max) + jnp.sum(jnp.exp(z - run_max), axis=0)
 
     def w_wait(s):
         for p in range(W_PIECES):
             w_copy(s, p).wait()
 
     last = len(steps) - 1
-    for j in steps[0]:
-        relay(j)
-    for k, j in enumerate(steps[0]):
-        arrived(j)
-        prepare(j, k, 0)
+    mid = vocab // 2
+    def first_rows(i):
+        prepare(steps[i][1], 1, i % 2)
+        multiply(i, 0, mid, 0, CW)
+        return multiply(i, 0, mid, CW, WK)
+
+    def other_rows(i):
+        prepare(steps[i + 1][0], 0, (i + 1) % 2)
+        multiply(i, mid, vocab - mid)
+
+    arrived(0)
+    prepare(0, 0, 0)
+    relay(1)
     w_wait(0)
-    pending = [j for cols in steps[1:] for j in cols]
     for i in range(last):
-        cols, nxt = steps[i], steps[i + 1]
-        cut_1, cut_2 = CUTS[len(cols)]
-        piece(i, 0, cut_1)
-        for j in nxt:
-            if j in pending:
-                relay(j)
-                pending.remove(j)
-        piece(i, cut_1, cut_2)
-        if len(nxt) == 1 and i + 2 <= last:
-            for j in steps[i + 2]:
-                relay(j)
-                pending.remove(j)
-        for j in nxt:
-            arrived(j)
-
-        def prepare_next():
-            for k, j in enumerate(nxt):
-                prepare(j, k, (i + 1) % 2)
-
-        piece(i, cut_2, vocab, prepare_next)
-        s = cols[0] // per_w
-        if nxt[0] // per_w != s:
-            if s + W_SLOTS < n_w:
-                for p in range(W_PIECES):
-                    w_copy(s + W_SLOTS, p).start(priority=1)
-            w_wait(s + 1)
-    low = jnp.full((lanes, n_req), -jnp.inf, jnp.float32)
-    run_max, = alone(lambda m: (highest(multiply(last, EDGES[0], EDGES[1]), m),), low)
-    ref, run_sum = run_max, jnp.zeros((lanes, n_req), jnp.float32)
-    for k in range(1, len(EDGES) - 1):
-        def final(run_max, ref, run_sum):
-            z = multiply(last, EDGES[k], EDGES[k + 1] - EDGES[k])
-            run_sum = add_up(EDGES[k - 1], EDGES[k], run_max, ref, run_sum)
-            return highest(z, run_max), run_max, run_sum
-
-        run_max, ref, run_sum = alone(final, run_max, ref, run_sum)
-    run_sum = add_up(EDGES[-2], EDGES[-1], run_max, ref, run_sum)
+        nxt = steps[i + 1]
+        arrived(steps[i][1])
+        relay(nxt[0])
+        alone(lambda: (first_rows(i), ())[1])
+        relay(nxt[1])
+        arrived(nxt[0])
+        alone(lambda: (other_rows(i), ())[1])
+        if i + W_SLOTS < n_w:
+            for p in range(W_PIECES):
+                w_copy(i + W_SLOTS, p).start(priority=1)
+        w_wait(i + 1)
+    arrived(steps[last][1])
+    run_max = jnp.full((lanes, n_req), -jnp.inf, jnp.float32)
+    ref, = alone(lambda m: (highest(first_rows(last), m),), run_max)
+
+    def add_up(k, run_sum, top):
+        z = logits_ref[pl.ds(pl.multiple_of(k * LAST, lanes), LAST), :]
+        return run_sum + jnp.sum(jnp.exp(z.reshape(LAST // lanes, lanes, n_req) - top), axis=0)
+
+    def second(ref):
+        run_max = highest(multiply(last, mid, vocab - mid), ref)
+        run_sum = jnp.zeros((lanes, n_req), jnp.float32)
+        for k in range(mid // LAST):
+            run_sum = add_up(k, run_sum, ref)
+        return run_max, run_sum * jnp.exp(ref - run_max)
+
+    run_max, run_sum = lax.fori_loop(0, once, lambda k, c: second(ref), (run_max, run_max))
+    run_sum = lax.fori_loop(mid // LAST, vocab // LAST, lambda k, c: add_up(k, c, run_max), run_sum)
     local_max = jnp.max(run_max, axis=0, keepdims=True)
     stat_buf[me, 0:1, :] = local_max
     stat_buf[me, 1:2, :] = jnp.sum(run_sum * jnp.exp(run_max - local_max), axis=0, keepdims=True)

time: 44.5 us -> 42.6 us (0.957)
  Pallas kernels: 43.6 us -> 41.7 us
    pallas_call x1, Pallas kernels: 39.6 us -> 37.7 us  [body(): pl.pallas_call(gather_head_kernel, out_shape=(pltpu.VMEM((vocab, n_req),...]
where the time goes in v4:
time: 42.6 us; the launch traced here: 42.5 us
  Pallas kernels  41.7 us (98%)
  between operations  0.82 us (2%)
    pallas_call x1, Pallas kernels, body(): pl.pallas_call(gather_head_kernel, out_shape=(pltpu.VMEM((vocab, n_req),...  37.7 us
    pallas_call x1, Pallas kernels, body(): pl.pallas_call(finish_kernel, out_shape=(jax.ShapeDtypeStruct((vocab, n_r...  3.96 us

profile of v4, /device:TPU:0, one launch (start us, length us, event | category | flops | bytes accessed | tf_op | source)
XLA Modules:
  0.0 42.5 jit_solution(7374892842184415510)
XLA Ops:
  0.6 0.0 copy-start
  0.6 37.7 %gather_head.1 = (f32[8000,256]{1,0:T(8,128)S(1)}, f32[1,256]{1,0:T(1,128)S(1)}) custom-call(bf16[128,4096]{1,0:T(8,128)(2,1)} %hidden_ref.1, s32[1,256]{1,0:T(1,128)} %bitcast.9, f32[1,4096]{1,0:T(1,128)} %bitcast.8, bf16[8000,4096]{1,0:T(8,128)(2,1)} %bitcast.7), custom_call_target="tpu_custom_call" | custom-call | tf_op jit(solution)/shard_map/gather_head/pallas_call | solution.py:252
  38.4 0.0 copy-done
  38.4 4.0 %finish.1 = (f32[8000,256]{1,0:T(8,128)}, f32[1,256]{1,0:T(1,128)}) custom-call(f32[8000,256]{1,0:T(8,128)S(1)} %get-tuple-element.6.logits_ref, f32[1,256]{1,0:T(1,128)S(1)} %get-tuple-element.7.norm_ref, s32[1,256]{1,0:T(1,128)S(1)} %bitcast.6), custom_call_target="tpu_custom_call" | custom-call | tf_op jit(solution)/shard_map/finish/pallas_call | solution.py:275
Async XLA Ops:
  0.6 37.8 %copy-start = (s32[256]{0:T(256)S(1)}, s32[256]{0:T(256)}, u32[]{:S(2)}) copy-start(s32[256]{0:T(256)} %param.7) | copy-start | bytes 3076

commit v5 on v4

--- a/solution.py
+++ b/solution.py
@@ -12,6 +12,7 @@
 W_SLOTS = 5
 W_PIECES = 4
 ROWS_OUT = 1000
+FIRST = 5600
 LAST = 800
 
 
@@ -160,7 +161,8 @@
 
     last = len(steps) - 1
     mid = vocab // 2
-    def first_rows(i):
+
+    def first_rows(i, mid=mid):
         prepare(steps[i][1], 1, i % 2)
         multiply(i, 0, mid, 0, CW)
         return multiply(i, 0, mid, CW, WK)
@@ -187,21 +189,21 @@
         w_wait(i + 1)
     arrived(steps[last][1])
     run_max = jnp.full((lanes, n_req), -jnp.inf, jnp.float32)
-    ref, = alone(lambda m: (highest(first_rows(last), m),), run_max)
 
     def add_up(k, run_sum, top):
         z = logits_ref[pl.ds(pl.multiple_of(k * LAST, lanes), LAST), :]
         return run_sum + jnp.sum(jnp.exp(z.reshape(LAST // lanes, lanes, n_req) - top), axis=0)
 
     def second(ref):
-        run_max = highest(multiply(last, mid, vocab - mid), ref)
+        ref = highest(first_rows(last, FIRST), ref)
+        run_max = highest(multiply(last, FIRST, vocab - FIRST), ref)
         run_sum = jnp.zeros((lanes, n_req), jnp.float32)
-        for k in range(mid // LAST):
+        for k in range(FIRST // LAST):
             run_sum = add_up(k, run_sum, ref)
         return run_max, run_sum * jnp.exp(ref - run_max)
 
-    run_max, run_sum = lax.fori_loop(0, once, lambda k, c: second(ref), (run_max, run_max))
-    run_sum = lax.fori_loop(mid // LAST, vocab // LAST, lambda k, c: add_up(k, c, run_max), run_sum)
+    run_max, run_sum = lax.fori_loop(0, once, lambda k, c: second(c[0]), (run_max, run_max))
+    run_sum = lax.fori_loop(FIRST // LAST, vocab // LAST, lambda k, c: add_up(k, c, run_max), run_sum)
     local_max = jnp.max(run_max, axis=0, keepdims=True)
     stat_buf[me, 0:1, :] = local_max
     stat_buf[me, 1:2, :] = jnp.sum(run_sum * jnp.exp(run_max - local_max), axis=0, keepdims=True)
@@ -220,12 +222,13 @@
     norm_ref[...] = group_max + jnp.log(group_sum)
 
 
-def finish_kernel(logits_ref, norm_ref, flag_ref, out_ref, norm_out_ref, stage, sem):
+def finish_kernel(logits_ref, norm_ref, flag_ref, out_ref, norm_out_ref, stage, sem, norm_sem):
     vocab = logits_ref.shape[0]
     n = vocab // ROWS_OUT
     keep = flag_ref[...] == 1
     norm = norm_ref[...]
-    norm_out_ref[...] = norm
+    norm_copy = pltpu.make_async_copy(norm_ref, norm_out_ref, norm_sem)
+    norm_copy.start()
 
     def out_copy(m):
         at = pl.ds(m * ROWS_OUT, ROWS_OUT)
@@ -235,6 +238,7 @@
         at = pl.ds(m * ROWS_OUT, ROWS_OUT)
         stage[at, :] = jnp.where(keep, logits_ref[at, :] - norm, 0.0)
         out_copy(m).start()
+    norm_copy.wait()
     for m in range(n):
         out_copy(m).wait()
 
@@ -276,8 +280,8 @@
             finish_kernel,
             out_shape=(jax.ShapeDtypeStruct((vocab, n_req), f32), jax.ShapeDtypeStruct((1, n_req), f32)),
             in_specs=[vmem, vmem, vmem],
-            out_specs=(hbm, vmem),
-            scratch_shapes=[pltpu.VMEM((vocab, n_req), f32), dma((vocab // ROWS_OUT,))],
+            out_specs=(hbm, hbm),
+            scratch_shapes=[pltpu.VMEM((vocab, n_req), f32), dma((vocab // ROWS_OUT,)), dma(())],
             compiler_params=pltpu.CompilerParams(vmem_limit_bytes=20 * 1024 * 1024),
             name="finish",
         )(logits, norm, is_final.reshape(1, n_req))

time: 42.6 us -> 41.9 us (0.984)
  Pallas kernels: 41.7 us -> 41 us
    pallas_call x1, Pallas kernels: 3.96 us -> 3.42 us  [body(): pl.pallas_call(finish_kernel, out_shape=(jax.ShapeDtypeStruct((vocab, n_r...]
where the time goes in v5:
time: 41.9 us; the launch traced here: 41.8 us
  Pallas kernels  41 us (98%)
  between operations  0.82 us (2%)
    pallas_call x1, Pallas kernels, body(): pl.pallas_call(gather_head_kernel, out_shape=(pltpu.VMEM((vocab, n_req),...  37.6 us
    pallas_call x1, Pallas kernels, body(): pl.pallas_call(finish_kernel, out_shape=(jax.ShapeDtypeStruct((vocab, n_r...  3.42 us

profile of v5, /device:TPU:0, one launch (start us, length us, event | category | flops | bytes accessed | tf_op | source)
XLA Modules:
  0.0 41.8 jit_solution(17151013544513543787)
XLA Ops:
  0.6 0.0 copy-start
  0.6 37.6 %gather_head.1 = (f32[8000,256]{1,0:T(8,128)S(1)}, f32[1,256]{1,0:T(1,128)S(1)}) custom-call(bf16[128,4096]{1,0:T(8,128)(2,1)} %hidden_ref.1, s32[1,256]{1,0:T(1,128)} %bitcast.9, f32[1,4096]{1,0:T(1,128)} %bitcast.8, bf16[8000,4096]{1,0:T(8,128)(2,1)} %bitcast.7), custom_call_target="tpu_custom_call" | custom-call | tf_op jit(solution)/shard_map/gather_head/pallas_call | solution.py:256
  38.2 0.0 copy-done
  38.2 3.4 %finish.1 = (f32[8000,256]{1,0:T(8,128)}, f32[1,256]{1,0:T(1,128)}) custom-call(f32[8000,256]{1,0:T(8,128)S(1)} %get-tuple-element.6.logits_ref, f32[1,256]{1,0:T(1,128)S(1)} %get-tuple-element.7.norm_ref, s32[1,256]{1,0:T(1,128)S(1)} %bitcast.6), custom_call_target="tpu_custom_call" | custom-call | tf_op jit(solution)/shard_map/finish/pallas_call | solution.py:279
Async XLA Ops:
  0.6 37.6 %copy-start = (s32[256]{0:T(256)S(1)}, s32[256]{0:T(256)}, u32[]{:S(2)}) copy-start(s32[256]{0:T(256)} %param.7) | copy-start | bytes 3076

commit v6 on v5

--- a/solution.py
+++ b/solution.py
@@ -12,7 +12,7 @@
 W_SLOTS = 5
 W_PIECES = 4
 ROWS_OUT = 1000
-FIRST = 5600
+FIRST = 6400
 LAST = 800
 
 

time: 41.9 us -> 41.9 us (level)
  no operation moved by 1% of the time
where the time goes in v6:
time: 41.9 us; the launch traced here: 41.8 us
  Pallas kernels  40.9 us (98%)
  between operations  0.82 us (2%)
    pallas_call x1, Pallas kernels, body(): pl.pallas_call(gather_head_kernel, out_shape=(pltpu.VMEM((vocab, n_req),...  37.5 us
    pallas_call x1, Pallas kernels, body(): pl.pallas_call(finish_kernel, out_shape=(jax.ShapeDtypeStruct((vocab, n_r...  3.42 us

profile of v6, /device:TPU:0, one launch (start us, length us, event | category | flops | bytes accessed | tf_op | source)
XLA Modules:
  0.0 41.8 jit_solution(4894623661724653027)
XLA Ops:
  0.6 0.0 copy-start
  0.6 37.5 %gather_head.1 = (f32[8000,256]{1,0:T(8,128)S(1)}, f32[1,256]{1,0:T(1,128)S(1)}) custom-call(bf16[128,4096]{1,0:T(8,128)(2,1)} %hidden_ref.1, s32[1,256]{1,0:T(1,128)} %bitcast.9, f32[1,4096]{1,0:T(1,128)} %bitcast.8, bf16[8000,4096]{1,0:T(8,128)(2,1)} %bitcast.7), custom_call_target="tpu_custom_call" | custom-call | tf_op jit(solution)/shard_map/gather_head/pallas_call | solution.py:256
  38.2 0.0 copy-done
  38.2 3.4 %finish.1 = (f32[8000,256]{1,0:T(8,128)}, f32[1,256]{1,0:T(1,128)}) custom-call(f32[8000,256]{1,0:T(8,128)S(1)} %get-tuple-element.6.logits_ref, f32[1,256]{1,0:T(1,128)S(1)} %get-tuple-element.7.norm_ref, s32[1,256]{1,0:T(1,128)S(1)} %bitcast.6), custom_call_target="tpu_custom_call" | custom-call | tf_op jit(solution)/shard_map/finish/pallas_call | solution.py:279
Async XLA Ops:
  0.6 37.5 %copy-start = (s32[256]{0:T(256)S(1)}, s32[256]{0:T(256)}, u32[]{:S(2)}) copy-start(s32[256]{0:T(256)} %param.7) | copy-start | bytes 3076
